TPU v7x, 32 devices: a whole 2x2x4 slice. The times are simulated.
32 devices in a mesh: freq: 4 (over x, core), gblk: 8 (over z, y).
Axes of the slice: x: 2, y: 2, z: 4, core: 2. Of those that a mesh axis runs over, the one named last changes fastest.
Arguments:
- w_imag: bfloat16 [8, 8192, 16384], P('freq', 'gblk'), may hold values from -0.046875 to 0.046875
- w_real: bfloat16 [4, 8192, 16384], P('freq', 'gblk'), may hold values from -0.046875 to 0.046875
- pair_elements: bfloat16 [8192, 256], P('gblk'), may hold values from -0.75 to 0.75
- quad_weight: float32 [8, 128], P('freq'), may hold values from 0.1 to 1
- residue_freq: int32 [128], replicated, may hold values from 0 to 3
- owner_bands: int32 [128], replicated, may hold values from 0 to 127, each once
Outputs:
- sigma: float32 [128, 256], P(('freq', 'gblk'))
Inputs may be any that keep to these rules, and one draw needn't show every extreme that they name: `owner_bands`: each band appears once.
All inputs are finite; a program needn't handle non-finite values.
Results may differ from a plain program's by a relative error of at most 0.0003.
Values may be sent and summed in bfloat16 or wider, within the bound.
A program may use at most 192 MiB of HBM per device.

v0:
```python
import functools
import math

import jax
import jax.numpy as jnp
from jax import lax
from jax.experimental import pallas as pl
from jax.experimental.pallas import tpu as pltpu
from jax.sharding import PartitionSpec as P

MESH = pl.DeviceIdType.MESH
LANES = 256
BUFFERS = 3


def ring_position(index, n):
    z = index // 2
    return z + (index % 2) * (n - 1 - 2 * z)


def ring_index(position, n):
    low = (position < n // 2).astype(jnp.int32)
    return low * (2 * position) + (1 - low) * (2 * (n - 1 - position) + 1)


def self_energy_kernel(
    n, nf, pieces_half, tile,
    wi_hbm, wr_hbm, m_hbm, quad_ref, residue_ref, owner_ref, out_ref,
    wbuf, gath, left, weights, ubuf, acc, stage, inbox,
    w_sem, own_sem, ring_send, ring_recv, pair_send, pair_recv, out_send, out_recv,
):
    f = lax.axis_index("freq")
    me = lax.axis_index("gblk")
    pos = ring_position(me, n)
    core = f % 2
    fi, rows, width = wi_hbm.shape
    fr = wr_hbm.shape[0]
    g_count = width // 2
    bands = owner_ref.shape[1]
    piece_rows = gath.shape[2]
    per_block = rows // tile
    steps = n * per_block
    lag = min(2 * per_block, steps - 1)
    devices = n * nf
    mine = f * n + me

    def slot_of(k):
        d = (k + 1) // 2
        sign = 2 * (k % 2) - 1
        return lax.rem(pos - sign * d + 2 * n, n)

    def w_copies(t, slot):
        block = ring_index(slot_of(t // per_block), n)
        col = block * rows + (t % per_block) * tile
        copies = []
        for half in range(2):
            cols = pl.ds(pl.multiple_of(col + half * g_count, tile), tile)
            copies.append(pltpu.make_async_copy(
                wi_hbm.at[:, :, cols], wbuf.at[slot, half, pl.ds(0, fi)], w_sem.at[slot, half, 0]))
            copies.append(pltpu.make_async_copy(
                wr_hbm.at[:, :, cols], wbuf.at[slot, half, pl.ds(fi, fr)], w_sem.at[slot, half, 1]))
        return copies

    barrier = pltpu.get_barrier_semaphore()

    def greet(r, carry):
        other = lax.rem(mine + r, devices)
        pl.semaphore_signal(barrier, inc=1, device_id=(other // n, other % n), device_id_type=MESH)
        return carry

    lax.fori_loop(1, devices, greet, 0)

    own = [pltpu.make_async_copy(
        m_hbm.at[pl.ds(i * piece_rows, piece_rows)], gath.at[pos, i], own_sem.at[i])
        for i in range(2 * pieces_half)]
    for c in own:
        c.start()
    for t in range(min(BUFFERS - 1, steps)):
        for c in w_copies(t, t):
            c.start()

    onehot_t = (lax.broadcasted_iota(jnp.int32, (bands, bands), 0) == owner_ref[...]).astype(jnp.float32)
    onehot = jnp.transpose(onehot_t)
    first = f * fr
    for j in range(fi):
        weights[j] = jnp.sum(onehot * quad_ref[pl.ds(j, 1), :], axis=1, keepdims=True)
    for j in range(fr):
        row = (residue_ref[...] == first + j).astype(jnp.float32)
        weights[fi + j] = jnp.sum(onehot * row, axis=1, keepdims=True)
    acc[...] = jnp.zeros_like(acc)
    for c in own:
        c.wait()
    own_m = gath[pos].reshape(rows, 2 * bands)
    picker = onehot.astype(jnp.bfloat16)
    for half in range(2):
        left[pl.ds(half * bands, bands), :] = lax.dot_general(
            picker, own_m[:, half * bands:(half + 1) * bands], (((1,), (1,)), ((), ())),
            preferred_element_type=jnp.float32).astype(jnp.bfloat16)

    split = (pieces_half + 1) // 2

    def direction(k, q):
        if k == n - 1:
            return 1 if q < split or n == 2 else -1
        return 1 if k % 2 else -1

    def ring_copy(k, q, sending_slot, sign):
        to = ring_index(lax.rem(pos + sign + n, n), n)
        at = gath.at[sending_slot, core * pieces_half + q]
        return pltpu.make_async_remote_copy(
            src_ref=at, dst_ref=at, send_sem=ring_send.at[k, q], recv_sem=ring_recv.at[k, q],
            device_id=(f, to), device_id_type=MESH)

    def pair_copy(k, q, whose):
        at = gath.at[slot_of(k), whose * pieces_half + q]
        return pltpu.make_async_remote_copy(
            src_ref=at, dst_ref=at, send_sem=pair_send.at[k, q], recv_sem=pair_recv.at[k, q],
            device_id=(f + 1 - 2 * core, me), device_id_type=MESH)

    def outgoing():
        found = []
        for q in range(pieces_half):
            for k in range(1, n):
                sign = direction(k, q)
                if k <= 2 and (k < n - 1 or n == 2):
                    source = 0
                elif k < n - 1:
                    source = k - 2
                else:
                    source = n - 3 if sign == 1 else n - 2
                found.append((k, q, source, sign))
        return found

    sends = outgoing()

    def start_own():
        for k, q, source, sign in sends:
            if source == 0:
                ring_copy(k, q, pos, sign).start()

    def event(k, q):
        ring_copy(k, q, slot_of(k), direction(k, q)).wait_recv()
        for k2, q2, source, sign in sends:
            if source == k and q2 == q:
                ring_copy(k2, q, slot_of(k), sign).start()
        pair_copy(k, q, core).start()

    per_dir = max(1, (n // 2) * pieces_half - pieces_half // 2)
    events = {}
    for k in range(1, n):
        for q in range(pieces_half):
            if k == n - 1 and direction(k, q) == -1:
                m = (n // 2 - 1) * pieces_half + q - split
            else:
                m = ((k + 1) // 2 - 1) * pieces_half + q
            at = math.ceil(0.18 * steps + 0.65 * steps * (m + 1) / per_dir)
            at = max(1, min(at, steps - 1, lag + k * per_block))
            events.setdefault(at, []).append((m, k, q))

    def v_product(v):
        block = v // per_block
        count = tile // piece_rows
        rhs = gath[slot_of(block), pl.ds((v % per_block) * count, count)].reshape(tile, 2 * bands)
        return jnp.dot(ubuf[v], rhs, preferred_element_type=jnp.float32)

    def await_pair(k):
        for q in range(pieces_half):
            pair_copy(k, q, 1 - core).wait_recv()

    def step(t, with_v):
        slot = lax.rem(t, BUFFERS)
        ahead = t + BUFFERS - 1

        @pl.when(ahead < steps)
        def _():
            for c in w_copies(ahead, lax.rem(ahead, BUFFERS)):
                c.start()

        for at, group in sorted(events.items()):
            if (at >= lag) == with_v:
                @pl.when(t == at)
                def _(group=group):
                    for _m, k, q in sorted(group):
                        event(k, q)
        if with_v:
            for k in range(1, n):
                if lag + k * per_block < steps:
                    @pl.when(t == lag + k * per_block)
                    def _(k=k):
                        await_pair(k)
        for c in w_copies(t, slot):
            c.wait()
        if with_v:
            acc[...] += v_product(t - lag)
        lhs = left[...]
        ur = ui = None
        for j in range(fi + fr):
            tr = jnp.dot(lhs, wbuf[slot, 0, j], preferred_element_type=jnp.float32)
            ti = jnp.dot(lhs, wbuf[slot, 1, j], preferred_element_type=jnp.float32)
            w = weights[j]
            a = w * (tr[:bands] + ti[bands:])
            b = w * (ti[:bands] - tr[bands:])
            ur = a if ur is None else ur + a
            ui = b if ui is None else ui + b
        for i, value in enumerate((ur, ui)):
            high = value.astype(jnp.bfloat16)
            low = (value - high.astype(jnp.float32)).astype(jnp.bfloat16)
            ubuf[t, pl.ds(2 * i * bands, bands), :] = high
            ubuf[t, pl.ds((2 * i + 1) * bands, bands), :] = low

    step(0, False)
    pl.semaphore_wait(barrier, devices - 1)
    start_own()

    def early(t, carry):
        step(t, False)
        return carry

    def late(t, carry):
        step(t, True)
        return carry

    lax.fori_loop(1, lag, early, 0)
    lax.fori_loop(lag, steps, late, 0)

    for k in range(1, n):
        if lag + k * per_block >= steps:
            await_pair(k)
    total = acc[...]
    for v in range(steps - lag, steps):
        total = total + v_product(v)
    p = total[:bands] + total[bands:2 * bands]
    q = total[2 * bands:3 * bands] + total[3 * bands:]
    real = p[:, :bands] - q[:, bands:]
    imag = p[:, bands:] + q[:, :bands]
    share = out_ref.shape[0]
    for d in range(devices):
        stage[d, :, pl.ds(0, bands)] = real[d * share:(d + 1) * share]
        stage[d, :, pl.ds(bands, bands)] = imag[d * share:(d + 1) * share]

    def give(r, carry):
        other = lax.rem(mine + r, devices)
        pltpu.make_async_remote_copy(
            src_ref=stage.at[other], dst_ref=inbox.at[r - 1], send_sem=out_send, recv_sem=out_recv,
            device_id=(other // n, other % n), device_id_type=MESH).start()
        return carry

    lax.fori_loop(1, devices, give, 0)
    for k, q_, source, sign in sends:
        ring_copy(k, q_, pos if source == 0 else slot_of(source), sign).wait_send()
    for k in range(1, n):
        for q_ in range(pieces_half):
            pair_copy(k, q_, core).wait_send()
    pltpu.make_async_copy(inbox, inbox, out_recv).wait()
    out_ref[...] = stage[mine] + jnp.sum(inbox[...], axis=0)
    pltpu.make_async_copy(inbox, inbox, out_send).wait()


def on_device(n, nf, w_imag, w_real, pair_elements, quad_weight, residue_freq, owner_bands):
    fi, rows, width = w_imag.shape
    fr = w_real.shape[0]
    bands = owner_bands.shape[0]
    tile = min(512, rows)
    pieces_half = 2 if rows >= 1024 else 1
    piece_rows = rows // (2 * pieces_half)
    steps = n * (rows // tile)
    devices = n * nf
    share = bands // devices
    dma = pltpu.SemaphoreType.DMA
    anyspace = pl.BlockSpec(memory_space=pl.ANY)
    vmem = pl.BlockSpec(memory_space=pltpu.VMEM)
    flops = 2 * (fi + fr) * rows * width * 2 * bands
    return pl.pallas_call(
        functools.partial(self_energy_kernel, n, nf, pieces_half, tile),
        out_shape=jax.ShapeDtypeStruct((share, 2 * bands), jnp.float32),
        in_specs=[anyspace, anyspace, anyspace, vmem, vmem, vmem],
        out_specs=vmem,
        scratch_shapes=[
            pltpu.VMEM((BUFFERS, 2, fi + fr, rows, tile), jnp.bfloat16),
            pltpu.VMEM((n, 2 * pieces_half, piece_rows, 2 * bands), jnp.bfloat16),
            pltpu.VMEM((2 * bands, rows), jnp.bfloat16),
            pltpu.VMEM((fi + fr, bands, 1), jnp.float32),
            pltpu.VMEM((steps, 4 * bands, tile), jnp.bfloat16),
            pltpu.VMEM((4 * bands, 2 * bands), jnp.float32),
            pltpu.VMEM((devices, share, 2 * bands), jnp.float32),
            pltpu.VMEM((devices - 1, share, 2 * bands), jnp.float32),
            dma((BUFFERS, 2, 2)),
            dma((2 * pieces_half,)),
            dma((n, pieces_half)),
            dma((n, pieces_half)),
            dma((n, pieces_half)),
            dma((n, pieces_half)),
            dma,
            dma,
        ],
        compiler_params=pltpu.CompilerParams(
            collective_id=0, has_side_effects=True, vmem_limit_bytes=60 * 1024 * 1024),
        cost_estimate=pl.CostEstimate(
            flops=flops, bytes_accessed=(fi + fr) * rows * width * 2, transcendentals=0),
    )(w_imag, w_real, pair_elements, quad_weight,
      residue_freq.reshape(1, bands), owner_bands.reshape(1, bands))


def solution(mesh):
    placed = (
        P("freq", "gblk", None),
        P("freq", "gblk", None),
        P("gblk", None),
        P("freq", None),
        P(),
        P(),
    )
    body = functools.partial(on_device, mesh.shape["gblk"], mesh.shape["freq"])
    return jax.shard_map(
        body, mesh=mesh, in_specs=placed, out_specs=P(("freq", "gblk"), None), check_vma=False
    )
```

profile of v0, /device:TPU:0, one launch (start us, length us, event | category | flops | bytes accessed | tf_op | source)
XLA Modules:
  0.0 53.8 jit_solution(5946776549877727046)
XLA Ops:
  0.0 52.5 %shard_map.64 = f32[4,256]{1,0:T(4,128)} custom-call(bf16[2,1024,16384]{2,1,0:T(8,128)(2,1)} %wi_hbm.1, bf16[1,1024,16384]{2,1,0:T(8,128)(2,1)} %wr_hbm.1, bf16[1024,256]{1,0:T(8,128)(2,1)} %m_hbm.1, f32[2,128]{1,0:T(2,128)} %quad_ref.1, s32[1,128]{1,0:T(1,128)} %bitcast.2, s32[1,128]{1,0:T(1,128)} %bitcast.3), custom_call_target="tpu_custom_call" | custom-call | flops 25769803776 | bytes 100663296 | tf_op jit(solution)/shard_map/pallas_call | solution.py:273
  52.5 1.3 %copy.8 = f32[4,256]{1,0:T(4,128)} copy(f32[4,256]{1,0:T(4,128)} %shard_map.64) | data formatting | bytes 8192
where the time goes:
time: 54 us; the launch traced here: 53.8 us
  Pallas kernels  52.5 us (97%)
  local copies, waits for them, and re-layouts  1.28 us (2%)
    pallas_call x1, Pallas kernels, on_device(): pl.pallas_call(functools.partial(self_energy_kernel, n, nf, pieces_half,...  52.5 us
    unnamed x1, local copies, waits for them, and re-layouts  1.28 us

commit v1 on v0

v1 whole, which is shorter than its diff:
```python
import functools

import jax
import jax.numpy as jnp
from jax import lax
from jax.experimental import pallas as pl
from jax.experimental.pallas import tpu as pltpu
from jax.sharding import PartitionSpec as P

MESH = pl.DeviceIdType.MESH
EDGE = 256
UNITS = 2
BUFFERS = 3
POP_AT = 2


def ring_position(index, n):
    z = index // 2
    return z + (index % 2) * (n - 1 - 2 * z)


def ring_index(position, n):
    low = (position < n // 2).astype(jnp.int32)
    return low * (2 * position) + (1 - low) * (2 * (n - 1 - position) + 1)


class Plan:
    def __init__(self, n, nf, rows, g_count, jobs):
        assert n % 2 == 0 and n > 2 and rows % EDGE == 0 and g_count % (UNITS * EDGE) == 0
        self.n, self.nf, self.rows, self.jobs = n, nf, rows, jobs
        self.devices = n * nf
        self.tile = UNITS * EDGE
        self.steps = g_count // self.tile
        self.per_block = rows // EDGE
        assert self.per_block == 1 or self.per_block % UNITS == 0
        self.halves = 2 if rows >= 1024 else 1
        self.piece_rows = rows // (2 * self.halves)
        self.pieces = EDGE // self.piece_rows
        self.split = (self.halves + 1) // 2
        whole = (n // 2 - 1) * self.halves
        self.plus = whole + self.split
        self.minus = whole + self.halves - self.split
        self.whole = whole
        self.events = max(self.plus, self.minus)
        if self.steps >= 2 * self.events:
            self.num, self.den, self.first = 3, 2, 4
        else:
            self.num, self.den, self.first = 1, 1, 1
        at = [self.first + (m * self.num) // self.den for m in range(self.events)]
        self.looped = sum(1 for a in at if a < self.steps)
        self.at = at
        lag = 2
        for k in range(1, n):
            need = (k * self.per_block) // UNITS
            last = max(self.at[m] for m in range(self.events) if k in self.blocks_of(m))
            lag = max(lag, last + 2 - need)
        self.lag = min(lag, self.steps - 2)

    def blocks_of(self, m):
        found = []
        if m < self.plus:
            found.append(2 * (m // self.halves) + 1)
        if m < self.minus:
            found.append(min(2 * (m // self.halves) + 2, self.n - 1))
        return found


def self_energy_kernel(
    plan,
    wi_hbm, wr_hbm, m_hbm, quad_hbm, residue_hbm, owner_hbm, out_ref,
    wbuf, gath, left, weights, uacc, ubuf, quad_ref, residue_ref, owner_ref, stage, inbox,
    w_sem, own_sem, small_sem, ring_send, ring_recv, pair_send, pair_recv, out_send, out_recv,
):
    def body(*accs):
        run(
            plan, accs[:UNITS], (accs[UNITS:2 * UNITS], accs[2 * UNITS:3 * UNITS], accs[3 * UNITS:]),
            wi_hbm, wr_hbm, m_hbm, quad_hbm, residue_hbm, owner_hbm, out_ref,
            wbuf, gath, left, weights, uacc, ubuf, quad_ref, residue_ref, owner_ref, stage, inbox,
            w_sem, own_sem, small_sem, ring_send, ring_recv, pair_send, pair_recv, out_send, out_recv)

    shape = (EDGE, EDGE)
    pl.run_scoped(body, *[pltpu.ACC(i % UNITS)(shape, jnp.float32) for i in range(4 * UNITS)])


def run(
    plan, vacc, uaccs,
    wi_hbm, wr_hbm, m_hbm, quad_hbm, residue_hbm, owner_hbm, out_ref,
    wbuf, gath, left, weights, uacc, ubuf, quad_ref, residue_ref, owner_ref, stage, inbox,
    w_sem, own_sem, small_sem, ring_send, ring_recv, pair_send, pair_recv, out_send, out_recv,
):
    n, nf, rows, jobs = plan.n, plan.nf, plan.rows, plan.jobs
    halves, piece_rows, steps, lag = plan.halves, plan.piece_rows, plan.steps, plan.lag
    per_block, devices, split = plan.per_block, plan.devices, plan.split
    f = lax.axis_index("freq")
    me = lax.axis_index("gblk")
    pos = ring_position(me, n)
    core = f % 2
    fi = wi_hbm.shape[0]
    fr = wr_hbm.shape[0]
    g_count = wi_hbm.shape[2] // 2
    bands = owner_ref.shape[1]
    mine = f * n + me
    chunks = [(part, c) for part in range(2) for c in range(rows // EDGE)]

    def slot_of(k):
        d = (k + 1) // 2
        sign = 2 * (k % 2) - 1
        return lax.rem(pos - sign * d + 2 * n, n)

    def w_source(j, part, col, width):
        cols = pl.ds(pl.multiple_of(col + part * g_count, EDGE), width)
        return wi_hbm.at[j, :, cols] if j < fi else wr_hbm.at[j - fi, :, cols]

    def start_w(t, slot, j):
        for part in range(2):
            if per_block == 1:
                for q in range(UNITS):
                    col = ring_index(slot_of(UNITS * t + q), n) * rows
                    pltpu.make_async_copy(
                        w_source(j, part, col, EDGE),
                        wbuf.at[slot, j, part, :, pl.ds(q * EDGE, EDGE)], w_sem.at[slot, j]).start()
            else:
                trips = per_block // UNITS
                col = ring_index(slot_of(t // trips), n) * rows + (t % trips) * plan.tile
                pltpu.make_async_copy(
                    w_source(j, part, col, plan.tile), wbuf.at[slot, j, part], w_sem.at[slot, j]).start()

    def wait_w(slot, j):
        pltpu.make_async_copy(wbuf.at[slot, j], wbuf.at[slot, j], w_sem.at[slot, j]).wait()

    small = [
        pltpu.make_async_copy(owner_hbm, owner_ref, small_sem.at[0]),
        pltpu.make_async_copy(quad_hbm, quad_ref, small_sem.at[1]),
        pltpu.make_async_copy(residue_hbm, residue_ref, small_sem.at[2]),
    ]
    own = [pltpu.make_async_copy(
        m_hbm.at[pl.ds(i * piece_rows, piece_rows)], gath.at[pos, i], own_sem.at[i])
        for i in range(2 * halves)]
    for c in small + own:
        c.start()
    for t in range(min(BUFFERS, steps)):
        for j in range(jobs):
            start_w(t, t, j)

    barrier = pltpu.get_barrier_semaphore()

    def greet(r, carry):
        other = lax.rem(mine + r, devices)
        pl.semaphore_signal(barrier, inc=1, device_id=(other // n, other % n), device_id_type=MESH)
        return carry

    lax.fori_loop(1, devices, greet, 0)

    for acc in list(vacc) + [a for pair in uaccs for a in pair]:
        pltpu.matmul_pop(acc)
    uacc[...] = jnp.zeros_like(uacc)

    for c in small:
        c.wait()
    onehot_t = (lax.broadcasted_iota(jnp.int32, (bands, bands), 0) == owner_ref[...]).astype(jnp.float32)
    onehot = jnp.transpose(onehot_t)
    for j in range(jobs):
        if j < fi:
            row = quad_ref[pl.ds(j, 1), :]
        else:
            row = (residue_ref[...] == f * fr + (j - fi)).astype(jnp.float32)
        column = jnp.broadcast_to(jnp.sum(onehot * row, axis=1, keepdims=True), (bands, EDGE))
        weights[j, pl.ds(0, bands), :] = column
        weights[j, pl.ds(bands, bands), :] = column
    nothing = jnp.zeros_like(onehot)
    pick = (
        jnp.concatenate([jnp.concatenate([onehot, nothing], axis=1),
                         jnp.concatenate([nothing, 0.0 - onehot], axis=1)], axis=0).astype(jnp.bfloat16),
        jnp.concatenate([jnp.concatenate([nothing, onehot], axis=1),
                         jnp.concatenate([onehot, nothing], axis=1)], axis=0).astype(jnp.bfloat16),
    )

    def m_tile(slot, sub):
        return gath[slot, pl.ds(sub * plan.pieces, plan.pieces)].reshape(EDGE, 2 * bands)

    for c in own:
        c.wait()
    for c in range(rows // EDGE):
        q = c % UNITS
        pltpu.matmul_push_rhs(m_tile(pos, c), 0, q, transpose=True)
        pltpu.matmul_acc_lhs(uaccs[0][q], pick[0], load_staged_rhs=0)
        pltpu.matmul_acc_lhs(uaccs[1][q], pick[1])
        left[0, c] = pltpu.matmul_pop(uaccs[0][q]).astype(jnp.bfloat16)
        left[1, c] = pltpu.matmul_pop(uaccs[1][q]).astype(jnp.bfloat16)

    def ring_copy(k, q, sending_slot, sign):
        to = ring_index(lax.rem(pos + sign + n, n), n)
        at = gath.at[sending_slot, core * halves + q]
        return pltpu.make_async_remote_copy(
            src_ref=at, dst_ref=at, send_sem=ring_send.at[k, q], recv_sem=ring_recv.at[k, q],
            device_id=(f, to), device_id_type=MESH)

    def pair_copy(k, q, whose):
        at = gath.at[slot_of(k), whose * halves + q]
        return pltpu.make_async_remote_copy(
            src_ref=at, dst_ref=at, send_sem=pair_send.at[k, q], recv_sem=pair_recv.at[k, q],
            device_id=(f + 1 - 2 * core, me), device_id_type=MESH)

    def start_own():
        for q in range(halves):
            ring_copy(1, q, pos, 1).start()
            ring_copy(2, q, pos, -1).start()

    def event(m):
        def plus():
            k, q = 2 * (m // halves) + 1, m % halves
            ring_copy(k, q, slot_of(k), 1).wait_recv()

            @pl.when((k + 2 < n - 1) | ((k + 2 == n - 1) & (q < split)))
            def _():
                ring_copy(k + 2, q, slot_of(k), 1).start()

            pair_copy(k, q, core).start()

        def minus():
            last = jnp.int32(m >= plan.whole) if isinstance(m, int) else (m >= plan.whole).astype(jnp.int32)
            k = (1 - last) * (2 * (m // halves) + 2) + last * (n - 1)
            q = (1 - last) * (m % halves) + last * (split + m - plan.whole)
            ring_copy(k, q, slot_of(k), -1).wait_recv()

            @pl.when((k + 2 < n - 1) | ((k == n - 2) & (q >= split)))
            def _():
                further = (k == n - 2).astype(jnp.int32)
                ring_copy((1 - further) * (k + 2) + further * (n - 1), q, slot_of(k), -1).start()

            pair_copy(k, q, core).start()

        pl.when(m < plan.plus)(plus)
        pl.when(m < plan.minus)(minus)

    def await_pair(k):
        for q in range(halves):
            pair_copy(k, q, 1 - core).wait_recv()

    def await_for(v):
        if per_block == 1:
            for q in range(UNITS):
                @pl.when((v >= 0) & (UNITS * v + q > 0))
                def _(q=q):
                    await_pair(UNITS * v + q)
        else:
            @pl.when((v > 0) & ((UNITS * v) % per_block == 0))
            def _():
                await_pair((UNITS * v) // per_block)

    def fence(t, j, final):
        slot = lax.rem(t, BUFFERS)
        if j < jobs - 1:
            wait_w(slot, j + 1)
        elif not final:
            wait_w(lax.rem(t + 1, BUFFERS), 0)

        if not final:
            @pl.when(t + BUFFERS < steps)
            def _():
                start_w(t + BUFFERS, slot, j)

        if j == jobs - 1:
            d = t - plan.first
            m = (d * plan.den + plan.num - 1) // plan.num
            pl.when((d >= 0) & ((m * plan.num) // plan.den == d) & (m < plan.events))(lambda: event(m))
            if not final:
                await_for(t + 1 - lag)

    def push_w(slot, j, part, c):
        for q in range(UNITS):
            pltpu.matmul_push_rhs(
                wbuf[slot, j, part, pl.ds(c * EDGE, EDGE), pl.ds(q * EDGE, EDGE)], 0, q)

    def push_v(v):
        for q in range(UNITS):
            i = UNITS * v + q
            pltpu.matmul_push_rhs(m_tile(slot_of(i // per_block), i % per_block), 0, q)

    def finish(t, j):
        for q in range(UNITS):
            value = weights[j] * pltpu.matmul_pop(uaccs[j % 3][q])
            if j > 0:
                value = uacc[q] + value
            if j < jobs - 1:
                uacc[q] = value
            else:
                high = value.astype(jnp.bfloat16)
                ubuf[t + 1, q, 0] = high
                ubuf[t + 1, q, 1] = (value - high.astype(jnp.float32)).astype(jnp.bfloat16)

    def v_part(v, part):
        for q in range(UNITS):
            pltpu.matmul_acc_lhs(vacc[q], ubuf[v + 1, q, part], load_staged_rhs=None if part else 0)

    def step(t, with_v, final=False):
        slot = lax.rem(t, BUFFERS)
        following = lax.rem(t + 1, BUFFERS)
        v = t - lag
        for j in range(jobs):
            for i, (part, c) in enumerate(chunks):
                end = i == len(chunks) - 1
                if end and (j < jobs - 1 or not with_v):
                    fence(t, j, final)
                lhs = left[part, c]
                for q in range(UNITS):
                    pltpu.matmul_acc_lhs(uaccs[j % 3][q], lhs, load_staged_rhs=0)
                if not end:
                    push_w(slot, j, *chunks[i + 1])
                elif j < jobs - 1:
                    push_w(slot, j + 1, *chunks[0])
                elif with_v:
                    push_v(v)
                else:
                    push_w(following, 0, *chunks[0])
                if i == min(POP_AT, len(chunks) - 1):
                    if j == 0:
                        finish(t - 1, jobs - 1)
                    else:
                        finish(t, j - 1)
        if with_v:
            fence(t, jobs - 1, final)
            v_part(v, 0)
            if not final:
                push_w(following, 0, *chunks[0])
            v_part(v, 1)

    wait_w(0, 0)
    push_w(0, 0, *chunks[0])

    def early(t, carry):
        @pl.when(t == 1)
        def _():
            pl.semaphore_wait(barrier, devices - 1)
            start_own()

        step(t, False)
        return carry

    def late(t, carry):
        step(t, True)
        return carry

    lax.fori_loop(0, lag, early, 0)
    lax.fori_loop(lag, steps - 1, late, 0)
    step(jnp.int32(steps - 1), True, final=True)
    for m in range(plan.events):
        if plan.at[m] >= steps:
            event(m)
    waited = set()
    for v in range(steps - lag, steps):
        if v == steps - 1:
            finish(steps - 1, jobs - 1)
        for q in range(UNITS):
            k, sub = (UNITS * v + q) // per_block, (UNITS * v + q) % per_block
            if sub == 0 and k > 0 and k not in waited:
                waited.add(k)
                await_pair(k)
        push_v(v)
        v_part(v, 0)
        v_part(v, 1)

    total = pltpu.matmul_pop(vacc[0]) + pltpu.matmul_pop(vacc[1])
    p = total[:bands]
    r = total[bands:]
    real = p[:, :bands] - r[:, bands:]
    imag = p[:, bands:] + r[:, :bands]
    share = out_ref.shape[0]
    for d in range(devices):
        stage[d, :, pl.ds(0, bands)] = real[d * share:(d + 1) * share]
        stage[d, :, pl.ds(bands, bands)] = imag[d * share:(d + 1) * share]

    def give(r, carry):
        other = lax.rem(mine + r, devices)
        pltpu.make_async_remote_copy(
            src_ref=stage.at[other], dst_ref=inbox.at[r - 1], send_sem=out_send, recv_sem=out_recv,
            device_id=(other // n, other % n), device_id_type=MESH).start()
        return carry

    lax.fori_loop(1, devices, give, 0)
    for q in range(halves):
        for k in range(1, n):
            forward = k % 2 == 1 if k < n - 1 else q < split
            if k <= 2:
                source = pos
            elif k < n - 1:
                source = slot_of(k - 2)
            else:
                source = slot_of(n - 3 if forward else n - 2)
            ring_copy(k, q, source, 1 if forward else -1).wait_send()
            pair_copy(k, q, core).wait_send()
    pltpu.make_async_copy(inbox, inbox, out_recv).wait()
    out_ref[...] = stage[mine] + jnp.sum(inbox[...], axis=0)
    pltpu.make_async_copy(inbox, inbox, out_send).wait()


def on_device(n, nf, w_imag, w_real, pair_elements, quad_weight, residue_freq, owner_bands):
    fi, rows, width = w_imag.shape
    fr = w_real.shape[0]
    bands = owner_bands.shape[0]
    jobs = fi + fr
    plan = Plan(n, nf, rows, width // 2, jobs)
    devices = n * nf
    share = bands // devices
    dma = pltpu.SemaphoreType.DMA
    anyspace = pl.BlockSpec(memory_space=pl.ANY)
    vmem = pl.BlockSpec(memory_space=pltpu.VMEM)
    flops = 2 * jobs * rows * width * 2 * bands
    halves = plan.halves
    return pl.pallas_call(
        functools.partial(self_energy_kernel, plan),
        out_shape=jax.ShapeDtypeStruct((share, 2 * bands), jnp.float32),
        in_specs=[anyspace] * 6,
        out_specs=vmem,
        scratch_shapes=[
            pltpu.VMEM((BUFFERS, jobs, 2, rows, plan.tile), jnp.bfloat16),
            pltpu.VMEM((n, 2 * halves, plan.piece_rows, 2 * bands), jnp.bfloat16),
            pltpu.VMEM((2, rows // EDGE, 2 * bands, EDGE), jnp.bfloat16),
            pltpu.VMEM((jobs, 2 * bands, EDGE), jnp.float32),
            pltpu.VMEM((UNITS, 2 * bands, EDGE), jnp.float32),
            pltpu.VMEM((plan.steps + 1, UNITS, 2, 2 * bands, EDGE), jnp.bfloat16),
            pltpu.VMEM((fi, bands), jnp.float32),
            pltpu.VMEM((1, bands), jnp.int32),
            pltpu.VMEM((1, bands), jnp.int32),
            pltpu.VMEM((devices, share, 2 * bands), jnp.float32),
            pltpu.VMEM((devices - 1, share, 2 * bands), jnp.float32),
            dma((BUFFERS, jobs)),
            dma((2 * halves,)),
            dma((3,)),
            dma((n, halves)),
            dma((n, halves)),
            dma((n, halves)),
            dma((n, halves)),
            dma,
            dma,
        ],
        compiler_params=pltpu.CompilerParams(
            collective_id=0, has_side_effects=True, vmem_limit_bytes=60 * 1024 * 1024),
        cost_estimate=pl.CostEstimate(
            flops=flops, bytes_accessed=jobs * rows * width * 2, transcendentals=0),
    )(w_imag, w_real, pair_elements, quad_weight,
      residue_freq.reshape(1, bands), owner_bands.reshape(1, bands))


def solution(mesh):
    placed = (
        P("freq", "gblk", None),
        P("freq", "gblk", None),
        P("gblk", None),
        P("freq", None),
        P(),
        P(),
    )
    body = functools.partial(on_device, mesh.shape["gblk"], mesh.shape["freq"])
    return jax.shard_map(
        body, mesh=mesh, in_specs=placed, out_specs=P(("freq", "gblk"), None), check_vma=False
    )
```

time: 54 us -> 48.5 us (0.90)
  Pallas kernels: 52.5 us -> 47 us
    pallas_call x1, Pallas kernels: 52.5 us -> 47 us  [on_device(): pl.pallas_call(functools.partial(self_energy_kernel, plan), out_shape=jax...]
where the time goes in v1:
time: 48.5 us; the launch traced here: 48.3 us
  Pallas kernels  47 us (97%)
  local copies, waits for them, and re-layouts  1.28 us (3%)
    pallas_call x1, Pallas kernels, on_device(): pl.pallas_call(functools.partial(self_energy_kernel, plan), out_shape=jax...  47 us
    unnamed x1, local copies, waits for them, and re-layouts  1.28 us

profile of v1, /device:TPU:0, one launch (start us, length us, event | category | flops | bytes accessed | tf_op | source)
XLA Modules:
  0.0 48.3 jit_solution(15276688171152787854)
XLA Ops:
  0.0 47.0 %shard_map.64 = f32[4,256]{1,0:T(4,128)} custom-call(bf16[2,1024,16384]{2,1,0:T(8,128)(2,1)} %wi_hbm.1, bf16[1,1024,16384]{2,1,0:T(8,128)(2,1)} %wr_hbm.1, bf16[1024,256]{1,0:T(8,128)(2,1)} %m_hbm.1, f32[2,128]{1,0:T(2,128)} %quad_hbm.1, s32[1,128]{1,0:T(1,128)} %bitcast.2, s32[1,128]{1,0:T(1,128)} %bitcast.3), custom_call_target="tpu_custom_call" | custom-call | flops 25769803776 | bytes 100663296 | tf_op jit(solution)/shard_map/pallas_call | solution.py:410
  47.0 1.3 %copy.8 = f32[4,256]{1,0:T(4,128)} copy(f32[4,256]{1,0:T(4,128)} %shard_map.64) | data formatting | bytes 8192

commit v2 on v1

--- a/solution.py
+++ b/solution.py
@@ -12,6 +12,7 @@
 UNITS = 2
 BUFFERS = 3
 POP_AT = 2
+FIRST = 2
 
 
 def ring_position(index, n):
@@ -26,7 +27,7 @@
 
 class Plan:
     def __init__(self, n, nf, rows, g_count, jobs):
-        assert n % 2 == 0 and n > 2 and rows % EDGE == 0 and g_count % (UNITS * EDGE) == 0
+        assert n % 2 == 0 and n > 2 and nf == 4 and rows % EDGE == 0 and g_count % (UNITS * EDGE) == 0
         self.n, self.nf, self.rows, self.jobs = n, nf, rows, jobs
         self.devices = n * nf
         self.tile = UNITS * EDGE
@@ -42,13 +43,11 @@
         self.minus = whole + self.halves - self.split
         self.whole = whole
         self.events = max(self.plus, self.minus)
-        if self.steps >= 2 * self.events:
-            self.num, self.den, self.first = 3, 2, 4
-        else:
-            self.num, self.den, self.first = 1, 1, 1
-        at = [self.first + (m * self.num) // self.den for m in range(self.events)]
-        self.looped = sum(1 for a in at if a < self.steps)
-        self.at = at
+        self.group = -(-self.events // 7)
+        self.rounds = -(-self.events // self.group)
+        self.num, self.den, self.first = 3, 2, FIRST * self.steps // 16
+        self.at = [self.first + ((m // self.group) * self.num) // self.den for m in range(self.events)]
+        assert self.at[-1] <= self.steps - 3
         lag = 2
         for k in range(1, n):
             need = (k * self.per_block) // UNITS
@@ -69,14 +68,14 @@
     plan,
     wi_hbm, wr_hbm, m_hbm, quad_hbm, residue_hbm, owner_hbm, out_ref,
     wbuf, gath, left, weights, uacc, ubuf, quad_ref, residue_ref, owner_ref, stage, inbox,
-    w_sem, own_sem, small_sem, ring_send, ring_recv, pair_send, pair_recv, out_send, out_recv,
+    w_sem, own_sem, small_sem, ring_send, ring_recv, pair_send, pair_recv, out_send, out_recv, plane_sem,
 ):
     def body(*accs):
         run(
             plan, accs[:UNITS], (accs[UNITS:2 * UNITS], accs[2 * UNITS:3 * UNITS], accs[3 * UNITS:]),
             wi_hbm, wr_hbm, m_hbm, quad_hbm, residue_hbm, owner_hbm, out_ref,
             wbuf, gath, left, weights, uacc, ubuf, quad_ref, residue_ref, owner_ref, stage, inbox,
-            w_sem, own_sem, small_sem, ring_send, ring_recv, pair_send, pair_recv, out_send, out_recv)
+            w_sem, own_sem, small_sem, ring_send, ring_recv, pair_send, pair_recv, out_send, out_recv, plane_sem)
 
     shape = (EDGE, EDGE)
     pl.run_scoped(body, *[pltpu.ACC(i % UNITS)(shape, jnp.float32) for i in range(4 * UNITS)])
@@ -86,7 +85,7 @@
     plan, vacc, uaccs,
     wi_hbm, wr_hbm, m_hbm, quad_hbm, residue_hbm, owner_hbm, out_ref,
     wbuf, gath, left, weights, uacc, ubuf, quad_ref, residue_ref, owner_ref, stage, inbox,
-    w_sem, own_sem, small_sem, ring_send, ring_recv, pair_send, pair_recv, out_send, out_recv,
+    w_sem, own_sem, small_sem, ring_send, ring_recv, pair_send, pair_recv, out_send, out_recv, plane_sem,
 ):
     n, nf, rows, jobs = plan.n, plan.nf, plan.rows, plan.jobs
     halves, piece_rows, steps, lag = plan.halves, plan.piece_rows, plan.steps, plan.lag
@@ -118,12 +117,12 @@
                     col = ring_index(slot_of(UNITS * t + q), n) * rows
                     pltpu.make_async_copy(
                         w_source(j, part, col, EDGE),
-                        wbuf.at[slot, j, part, :, pl.ds(q * EDGE, EDGE)], w_sem.at[slot, j]).start()
+                        wbuf.at[slot, j, part, :, pl.ds(q * EDGE, EDGE)], w_sem.at[slot, j]).start(priority=1)
             else:
                 trips = per_block // UNITS
                 col = ring_index(slot_of(t // trips), n) * rows + (t % trips) * plan.tile
                 pltpu.make_async_copy(
-                    w_source(j, part, col, plan.tile), wbuf.at[slot, j, part], w_sem.at[slot, j]).start()
+                    w_source(j, part, col, plan.tile), wbuf.at[slot, j, part], w_sem.at[slot, j]).start(priority=1)
 
     def wait_w(slot, j):
         pltpu.make_async_copy(wbuf.at[slot, j], wbuf.at[slot, j], w_sem.at[slot, j]).wait()
@@ -144,12 +143,11 @@
 
     barrier = pltpu.get_barrier_semaphore()
 
-    def greet(r, carry):
-        other = lax.rem(mine + r, devices)
-        pl.semaphore_signal(barrier, inc=1, device_id=(other // n, other % n), device_id_type=MESH)
-        return carry
-
-    lax.fori_loop(1, devices, greet, 0)
+    pair = (f + 1 - 2 * core, me)
+    twin = (lax.rem(f + 2, nf), me)
+    near = [(f, ring_index(lax.rem(pos + 1, n), n)), (f, ring_index(lax.rem(pos + n - 1, n), n)), pair, twin]
+    for other in near:
+        pl.semaphore_signal(barrier, inc=1, device_id=other, device_id_type=MESH)
 
     for acc in list(vacc) + [a for pair in uaccs for a in pair]:
         pltpu.matmul_pop(acc)
@@ -178,8 +176,28 @@
     def m_tile(slot, sub):
         return gath[slot, pl.ds(sub * plan.pieces, plan.pieces)].reshape(EDGE, 2 * bands)
 
+    def ring_copy(k, q, sending_slot, sign):
+        to = ring_index(lax.rem(pos + sign + n, n), n)
+        at = gath.at[sending_slot, core * halves + q]
+        return pltpu.make_async_remote_copy(
+            src_ref=at, dst_ref=at, send_sem=ring_send.at[k, q], recv_sem=ring_recv.at[k, q],
+            device_id=(f, to), device_id_type=MESH)
+
+    def pair_copy(k, q, whose):
+        at = gath.at[slot_of(k), whose * halves + q]
+        return pltpu.make_async_remote_copy(
+            src_ref=at, dst_ref=at, send_sem=pair_send.at[k, q], recv_sem=pair_recv.at[k, q],
+            device_id=(f + 1 - 2 * core, me), device_id_type=MESH)
+
+    def start_own():
+        for q in range(halves):
+            ring_copy(1, q, pos, 1).start()
+            ring_copy(2, q, pos, -1).start()
+
     for c in own:
         c.wait()
+    pl.semaphore_wait(barrier, len(near))
+    start_own()
     for c in range(rows // EDGE):
         q = c % UNITS
         pltpu.matmul_push_rhs(m_tile(pos, c), 0, q, transpose=True)
@@ -187,24 +205,6 @@
         pltpu.matmul_acc_lhs(uaccs[1][q], pick[1])
         left[0, c] = pltpu.matmul_pop(uaccs[0][q]).astype(jnp.bfloat16)
         left[1, c] = pltpu.matmul_pop(uaccs[1][q]).astype(jnp.bfloat16)
-
-    def ring_copy(k, q, sending_slot, sign):
-        to = ring_index(lax.rem(pos + sign + n, n), n)
-        at = gath.at[sending_slot, core * halves + q]
-        return pltpu.make_async_remote_copy(
-            src_ref=at, dst_ref=at, send_sem=ring_send.at[k, q], recv_sem=ring_recv.at[k, q],
-            device_id=(f, to), device_id_type=MESH)
-
-    def pair_copy(k, q, whose):
-        at = gath.at[slot_of(k), whose * halves + q]
-        return pltpu.make_async_remote_copy(
-            src_ref=at, dst_ref=at, send_sem=pair_send.at[k, q], recv_sem=pair_recv.at[k, q],
-            device_id=(f + 1 - 2 * core, me), device_id_type=MESH)
-
-    def start_own():
-        for q in range(halves):
-            ring_copy(1, q, pos, 1).start()
-            ring_copy(2, q, pos, -1).start()
 
     def event(m):
         def plus():
@@ -260,12 +260,17 @@
             def _():
                 start_w(t + BUFFERS, slot, j)
 
-        if j == jobs - 1:
+        if j == jobs - 1 and not final:
             d = t - plan.first
-            m = (d * plan.den + plan.num - 1) // plan.num
-            pl.when((d >= 0) & ((m * plan.num) // plan.den == d) & (m < plan.events))(lambda: event(m))
-            if not final:
-                await_for(t + 1 - lag)
+            e = (d * plan.den + plan.num - 1) // plan.num
+            due = (d >= 0) & ((e * plan.num) // plan.den == d) & (e < plan.rounds)
+
+            def act(i, carry):
+                event(e * plan.group + i)
+                return carry
+
+            lax.fori_loop(0, plan.group * due.astype(jnp.int32), act, 0)
+            await_for(t + 1 - lag)
 
     def push_w(slot, j, part, c):
         for q in range(UNITS):
@@ -297,10 +302,12 @@
         slot = lax.rem(t, BUFFERS)
         following = lax.rem(t + 1, BUFFERS)
         v = t - lag
+        left_over = list(range(steps - 1 - lag, steps - 2))
+        share = -(-len(left_over) // (jobs - 1))
         for j in range(jobs):
             for i, (part, c) in enumerate(chunks):
                 end = i == len(chunks) - 1
-                if end and (j < jobs - 1 or not with_v):
+                if end and not final and (j < jobs - 1 or not with_v):
                     fence(t, j, final)
                 lhs = left[part, c]
                 for q in range(UNITS):
@@ -308,7 +315,15 @@
                 if not end:
                     push_w(slot, j, *chunks[i + 1])
                 elif j < jobs - 1:
+                    if final:
+                        for extra in left_over[j * share:(j + 1) * share]:
+                            push_v(extra)
+                            v_part(extra, 0)
+                            v_part(extra, 1)
+                        fence(t, j, final)
                     push_w(slot, j + 1, *chunks[0])
+                elif final:
+                    push_v(steps - 2)
                 elif with_v:
                     push_v(v)
                 else:
@@ -318,22 +333,19 @@
                         finish(t - 1, jobs - 1)
                     else:
                         finish(t, j - 1)
-        if with_v:
+        if final:
+            v_part(steps - 2, 0)
+            v_part(steps - 2, 1)
+        elif with_v:
             fence(t, jobs - 1, final)
             v_part(v, 0)
-            if not final:
-                push_w(following, 0, *chunks[0])
+            push_w(following, 0, *chunks[0])
             v_part(v, 1)
 
     wait_w(0, 0)
     push_w(0, 0, *chunks[0])
 
     def early(t, carry):
-        @pl.when(t == 1)
-        def _():
-            pl.semaphore_wait(barrier, devices - 1)
-            start_own()
-
         step(t, False)
         return carry
 
@@ -343,22 +355,14 @@
 
     lax.fori_loop(0, lag, early, 0)
     lax.fori_loop(lag, steps - 1, late, 0)
+    for v in range(steps - lag, steps):
+        await_for(jnp.int32(v))
+    pl.semaphore_signal(plane_sem, inc=1, device_id=twin, device_id_type=MESH)
     step(jnp.int32(steps - 1), True, final=True)
-    for m in range(plan.events):
-        if plan.at[m] >= steps:
-            event(m)
-    waited = set()
-    for v in range(steps - lag, steps):
-        if v == steps - 1:
-            finish(steps - 1, jobs - 1)
-        for q in range(UNITS):
-            k, sub = (UNITS * v + q) // per_block, (UNITS * v + q) % per_block
-            if sub == 0 and k > 0 and k not in waited:
-                waited.add(k)
-                await_pair(k)
-        push_v(v)
-        v_part(v, 0)
-        v_part(v, 1)
+    finish(steps - 1, jobs - 1)
+    push_v(steps - 1)
+    v_part(steps - 1, 0)
+    v_part(steps - 1, 1)
 
     total = pltpu.matmul_pop(vacc[0]) + pltpu.matmul_pop(vacc[1])
     p = total[:bands]
@@ -377,6 +381,7 @@
             device_id=(other // n, other % n), device_id_type=MESH).start()
         return carry
 
+    pl.semaphore_wait(plane_sem, 1)
     lax.fori_loop(1, devices, give, 0)
     for q in range(halves):
         for k in range(1, n):
@@ -433,13 +438,15 @@
             dma((n, halves)),
             dma,
             dma,
+            pltpu.SemaphoreType.REGULAR,
         ],
         compiler_params=pltpu.CompilerParams(
-            collective_id=0, has_side_effects=True, vmem_limit_bytes=60 * 1024 * 1024),
+            collective_id=0, has_side_effects=True, vmem_limit_bytes=44 * 1024 * 1024),
         cost_estimate=pl.CostEstimate(
             flops=flops, bytes_accessed=jobs * rows * width * 2, transcendentals=0),
-    )(w_imag, w_real, pair_elements, quad_weight,
-      residue_freq.reshape(1, bands), owner_bands.reshape(1, bands))
+    )(*[pltpu.with_memory_space_constraint(x, pltpu.HBM) for x in (
+        w_imag, w_real, pair_elements, quad_weight,
+        residue_freq.reshape(1, bands), owner_bands.reshape(1, bands))])
 
 
 def solution(mesh):

time: 48.5 us -> 43 us (0.89)
  Pallas kernels: 47 us -> 42.3 us
  local copies, waits for them, and re-layouts: 1.28 us -> 0.6 us
    pallas_call x1, Pallas kernels: 47 us -> 42.3 us  [on_device(): pl.pallas_call(functools.partial(self_energy_kernel, plan), out_shape=jax...]
    unnamed x1, local copies, waits for them, and re-layouts: 1.28 us -> 0.6 us
where the time goes in v2:
time: 43 us; the launch traced here: 42.9 us
  Pallas kernels  42.3 us (98%)
  local copies, waits for them, and re-layouts  0.6 us (1%)
    pallas_call x1, Pallas kernels, on_device(): pl.pallas_call(functools.partial(self_energy_kernel, plan), out_shape=jax...  42.3 us

profile of v2, /device:TPU:0, one launch (start us, length us, event | category | flops | bytes accessed | tf_op | source)
XLA Modules:
  0.0 42.9 jit_solution(4051846289036240590)
XLA Ops:
  0.0 42.3 %shard_map.64 = f32[4,256]{1,0:T(4,128)S(1)} custom-call(bf16[2,1024,16384]{2,1,0:T(8,128)(2,1)} %wi_hbm.1, bf16[1,1024,16384]{2,1,0:T(8,128)(2,1)} %wr_hbm.1, bf16[1024,256]{1,0:T(8,128)(2,1)} %m_hbm.1, f32[2,128]{1,0:T(2,128)} %quad_hbm.1, s32[1,128]{1,0:T(1,128)} %bitcast.2, s32[1,128]{1,0:T(1,128)} %bitcast.3), custom_call_target="tpu_custom_call" | custom-call | flops 25769803776 | bytes 100663296 | tf_op jit(solution)/shard_map/pallas_call | solution.py:415
  42.3 0.6 %copy.8 = f32[4,256]{1,0:T(4,128)} copy(f32[4,256]{1,0:T(4,128)S(1)} %shard_map.64) | data formatting | bytes 8192

commit v3 on v2

--- a/solution.py
+++ b/solution.py
@@ -10,7 +10,7 @@
 MESH = pl.DeviceIdType.MESH
 EDGE = 256
 UNITS = 2
-BUFFERS = 3
+BUFFERS = 4
 POP_AT = 2
 FIRST = 2
 
@@ -374,15 +374,18 @@
         stage[d, :, pl.ds(0, bands)] = real[d * share:(d + 1) * share]
         stage[d, :, pl.ds(bands, bands)] = imag[d * share:(d + 1) * share]
 
-    def give(r, carry):
-        other = lax.rem(mine + r, devices)
+    deep = n // 2
+    order = [(df, dz, dy)
+             for dz in sorted(range(deep), key=lambda dz: -min(dz, deep - dz))
+             for df in (2, 1, 3, 0) for dy in (1, 0)]
+    order.remove((0, 0, 0))
+    pl.semaphore_wait(plane_sem, 1)
+    for i, (df, dz, dy) in enumerate(order):
+        other_f = lax.rem(f + df, nf)
+        other_g = 2 * lax.rem(me // 2 + dz, deep) + lax.rem(me % 2 + dy, 2)
         pltpu.make_async_remote_copy(
-            src_ref=stage.at[other], dst_ref=inbox.at[r - 1], send_sem=out_send, recv_sem=out_recv,
-            device_id=(other // n, other % n), device_id_type=MESH).start()
-        return carry
-
-    pl.semaphore_wait(plane_sem, 1)
-    lax.fori_loop(1, devices, give, 0)
+            src_ref=stage.at[other_f * n + other_g], dst_ref=inbox.at[i], send_sem=out_send, recv_sem=out_recv,
+            device_id=(other_f, other_g), device_id_type=MESH).start()
     for q in range(halves):
         for k in range(1, n):
             forward = k % 2 == 1 if k < n - 1 else q < split

time: 43 us -> 43.1 us (level)
  no operation moved by 1% of the time
where the time goes in v3:
time: 43.1 us; the launch traced here: 43 us
  Pallas kernels  42.4 us (98%)
  local copies, waits for them, and re-layouts  0.6 us (1%)
    pallas_call x1, Pallas kernels, on_device(): pl.pallas_call(functools.partial(self_energy_kernel, plan), out_shape=jax...  42.4 us

profile of v3, /device:TPU:0, one launch (start us, length us, event | category | flops | bytes accessed | tf_op | source)
XLA Modules:
  0.0 43.0 jit_solution(8012496775575665269)
XLA Ops:
  0.0 42.4 %shard_map.64 = f32[4,256]{1,0:T(4,128)S(1)} custom-call(bf16[2,1024,16384]{2,1,0:T(8,128)(2,1)} %wi_hbm.1, bf16[1,1024,16384]{2,1,0:T(8,128)(2,1)} %wr_hbm.1, bf16[1024,256]{1,0:T(8,128)(2,1)} %m_hbm.1, f32[2,128]{1,0:T(2,128)} %quad_hbm.1, s32[1,128]{1,0:T(1,128)} %bitcast.2, s32[1,128]{1,0:T(1,128)} %bitcast.3), custom_call_target="tpu_custom_call" | custom-call | flops 25769803776 | bytes 100663296 | tf_op jit(solution)/shard_map/pallas_call | solution.py:418
  42.4 0.6 %copy.8 = f32[4,256]{1,0:T(4,128)} copy(f32[4,256]{1,0:T(4,128)S(1)} %shard_map.64) | data formatting | bytes 8192
